TPU v7x, 256 devices: a whole 4x4x8 slice. The times are simulated.
256 devices in a mesh: grp: 4 (over y), dev: 64 (over z, x, core).
Axes of the slice: x: 4, y: 4, z: 8, core: 2. Of those that a mesh axis runs over, the one named last changes fastest.
Arguments:
- pool_latent: bfloat16 [512, 256, 512], P(('grp', 'dev')), may hold values from -6 to 6
- pool_rope: bfloat16 [512, 64, 256], P(('grp', 'dev')), may hold values from -6 to 6
- q_nope: bfloat16 [1024, 16384], P(None, 'dev'), may hold values from -6 to 6
- q_rope: bfloat16 [1024, 8192], P(None, 'dev'), may hold values from -9 to 9
- w_uk: bfloat16 [512, 16384], P(None, 'dev'), may hold values from -0.25 to 0.25
- w_uv: bfloat16 [512, 16384], P(None, 'dev'), may hold values from -0.25 to 0.25
- w_o: bfloat16 [16384, 7168], P('dev'), may hold values from -0.046875 to 0.046875
- block_table: int32 [64, 8], replicated, may hold values from 0 to 511, as said below
- lengths: int32 [64], replicated, may hold values from 2 to 2048, as said below
- preempted: int32 [32], replicated, may hold values from 0 to 63, as said below
- assignment: int32 [32], replicated, may hold values from 0 to 3, as said below
Outputs:
- mixed: bfloat16 [1024, 7168], P('grp', 'dev')
Inputs may be any that keep to these rules, and one draw needn't show every extreme that they name: `preempted`: distinct slots. `assignment`: each group receives exactly 8 requests. `block_table`: every page number 0 to 511 appears exactly once in the table; page p lies on the device with index p // 2 along grp+dev, at position p % 2 there. For every group and every index along dev, exactly 1 of the pages listed for the slots of that group's requests lie on devices with that index along dev. `lengths`: in every draw all requests of one group hold more than (7) * 256 tokens.
All inputs are finite; a program needn't handle non-finite values.
Results may differ from a plain program's by a relative error of at most 0.015.
Values may be sent and summed in bfloat16 or wider, within the bound.
No kernel may reach another device: no remote copies, remote signals or barrier semaphores. Data moves between devices by JAX's collectives and lax.ppermute only.
A program may use at most 128 MiB of HBM per device.

v0:
```python
import math
import jax
import jax.numpy as jnp
from jax import lax
from jax.sharding import Mesh
from jax.sharding import PartitionSpec as P

DR = 64
DN = 128
DV = 128
DEV = ("dev_0", "dev_1", "dev_2")
GRP_DEV = ("grp", "dev_0", "dev_1", "dev_2")
NEG = -1e30


def sent_together(arrays, axis, split_dim, concat_dim, along):
    widths = [math.prod(a.shape[along:]) for a in arrays]
    both = jnp.concatenate(
        [a.reshape(*a.shape[:along], w) for a, w in zip(arrays, widths)], axis=along
    )
    filled = lax.all_to_all(both, axis, split_axis=split_dim, concat_axis=concat_dim, tiled=True)
    tiles = jnp.split(filled, [sum(widths[:k]) for k in range(1, len(widths))], axis=along)
    return tuple(
        (b.reshape(*filled.shape[:along], *a.shape[along:]) for a, b in zip(arrays, tiles))
    )


def summed_rows(so_far, axes):
    for axis in axes:
        so_far = lax.psum_scatter(so_far, axis, scatter_dimension=0, tiled=True)
    return so_far


def place_values(targets, values, length, dtype):
    return jnp.zeros((length + 1,), dtype).at[targets].set(values)[:length]


def local(
    pool_latent,
    pool_rope,
    q_nope,
    q_rope,
    w_uk,
    w_uv,
    w_o,
    block_table,
    lengths,
    preempted,
    assignment,
):
    groups = lax.axis_size("grp")
    columns = lax.axis_size(DEV)
    group = lax.axis_index("grp")
    column = lax.axis_index(DEV)
    pages_dev = pool_latent.shape[0]
    block = pool_latent.shape[1]
    latent_width = pool_latent.shape[2]
    rope_width = pool_rope.shape[1]
    requests = preempted.shape[0]
    blocks = block_table.shape[1]
    per_group = requests // groups
    group_pages = per_group * blocks
    per_column = group_pages // columns
    query_rows = q_nope.shape[0] // requests
    heads_dev = q_rope.shape[1] // rope_width
    scale = 1.0 / math.sqrt(DN + DR)
    slot_pages = block_table[preempted]
    slot_len = lengths[preempted]
    req_ids = jnp.arange(requests, dtype=jnp.int32)
    earlier = (assignment[:, None] == assignment[None, :]) & (req_ids[None, :] < req_ids[:, None])
    rank = jnp.sum(earlier.astype(jnp.int32), axis=1)
    entries = requests * blocks
    entry_ids = jnp.arange(entries, dtype=jnp.int32)
    entry_page = slot_pages.reshape(entries)
    entry_req = entry_ids // blocks
    entry_block = entry_ids % blocks
    entry_group = assignment[entry_req]
    holder = entry_page // pages_dev
    entry_row = holder // columns
    entry_col = holder % columns
    entry_local = entry_page % pages_dev
    entry_key = entry_col * groups + entry_group
    before = (entry_key[:, None] == entry_key[None, :]) & (entry_ids[None, :] < entry_ids[:, None])
    entry_slot = jnp.sum(before.astype(jnp.int32), axis=1)
    entry_pos = entry_col * per_column + entry_slot
    entry_valid = jnp.clip(slot_len[entry_req] - entry_block * block, 0, block)
    outgoing = groups * per_column
    sending = (entry_row == group) & (entry_col == column)
    send_target = jnp.where(sending, entry_group * per_column + entry_slot, outgoing)
    send_index = place_values(send_target, entry_local, outgoing, jnp.int32)
    send_live = place_values(send_target, jnp.ones((entries,), jnp.bool_), outgoing, jnp.bool_)
    zero = jnp.zeros((), pool_latent.dtype)
    out_latent = jnp.where(send_live[:, None, None], pool_latent[send_index], zero)
    out_rope = jnp.where(send_live[:, None, None], pool_rope[send_index], zero)
    got_latent, got_rope = sent_together((out_latent, out_rope), "grp", 0, 0, 1)
    mine = (entry_group == group) & (entry_col == column)
    source = place_values(jnp.where(mine, entry_slot, per_column), entry_row, per_column, jnp.int32)
    pick = source * per_column + jnp.arange(per_column, dtype=jnp.int32)
    own_latent = got_latent[pick]
    own_rope = got_rope[pick]
    in_group = entry_group == group
    pos_target = jnp.where(in_group, entry_pos, group_pages)
    page_req = place_values(pos_target, rank[entry_req], group_pages, jnp.int32)
    page_valid = place_values(pos_target, entry_valid, group_pages, jnp.int32)
    members = place_values(
        jnp.where(assignment == group, rank, per_group), req_ids, per_group, jnp.int32
    )
    rows = (
        members[:, None] * query_rows + jnp.arange(query_rows, dtype=jnp.int32)[None, :]
    ).reshape(-1)
    query_lo = q_nope[rows].reshape(per_group * query_rows, heads_dev, DN)
    query_hi = q_rope[rows].reshape(per_group, query_rows, heads_dev, rope_width)
    w_key = w_uk.reshape(latent_width, heads_dev, DN)
    q_lat = jnp.einsum("qhn,chn->qhc", query_lo, w_key, preferred_element_type=jnp.float32).astype(
        jnp.bfloat16
    )
    q_lat = q_lat.reshape(per_group, query_rows, heads_dev, latent_width)
    request_ids = jnp.arange(per_group, dtype=jnp.int32)
    token_ids = jnp.arange(block, dtype=jnp.int32)
    start_top = jnp.full((per_group, query_rows, heads_dev), NEG, jnp.float32)
    latent_piece = lax.all_gather(own_latent, DEV, axis=0, tiled=True)
    rope_piece = lax.all_gather(own_rope, DEV, axis=0, tiled=True)
    score = jnp.einsum(
        "pqhc,pkc->pqhk", q_lat[page_req], latent_piece, preferred_element_type=jnp.float32
    )
    score = score + jnp.einsum(
        "pqhr,prk->pqhk", query_hi[page_req], rope_piece, preferred_element_type=jnp.float32
    )
    score = score * scale
    live = token_ids[None, None, None, :] < page_valid[:, None, None, None]
    score = jnp.where(live, score, NEG)
    onehot = page_req[:, None] == request_ids[None, :]
    page_top = jnp.max(score, axis=3)
    piece_top = jnp.max(jnp.where(onehot[:, :, None, None], page_top[:, None], NEG), axis=0)
    top_new = jnp.maximum(start_top, piece_top)
    expo = jnp.where(live, jnp.exp(score - top_new[page_req][..., None]), 0.0)
    select = onehot.astype(jnp.float32)
    total_new = jnp.einsum(
        "pr,pqh->rqh", select, jnp.sum(expo, axis=3), precision=lax.Precision.HIGHEST
    )
    values = jnp.einsum(
        "pqhk,pkc->pqhc",
        expo.astype(jnp.bfloat16),
        latent_piece,
        preferred_element_type=jnp.float32,
    )
    acc_new = jnp.einsum("pr,pqhc->rqhc", select, values, precision=lax.Precision.HIGHEST)
    o_lat = (
        (acc_new / total_new[..., None])
        .astype(jnp.bfloat16)
        .reshape(per_group * query_rows, heads_dev, latent_width)
    )
    w_val = w_uv.reshape(latent_width, heads_dev, DV)
    heads_out = jnp.einsum("qhc,chv->qhv", o_lat, w_val, preferred_element_type=jnp.float32).astype(
        jnp.bfloat16
    )
    heads_out = heads_out.reshape(per_group * query_rows, heads_dev * DV)
    mixed = summed_rows(
        lax.dot_general(
            w_o, heads_out, (((0,), (1,)), ((), ())), preferred_element_type=jnp.float32
        ),
        DEV,
    )
    return mixed.T.astype(jnp.bfloat16)


def solution(mesh):
    split = Mesh(
        mesh.devices.reshape(mesh.shape["grp"], 8, 4, 2), ("grp", "dev_0", "dev_1", "dev_2")
    )
    return jax.shard_map(
        local,
        mesh=split,
        in_specs=(
            P(GRP_DEV, None, None),
            P(GRP_DEV, None, None),
            P(None, DEV),
            P(None, DEV),
            P(None, DEV),
            P(None, DEV),
            P(DEV, None),
            P(),
            P(),
            P(),
            P(),
        ),
        out_specs=P("grp", DEV),
        check_vma=False,
    )
```

profile of v0, /device:TPU:1, one launch (start us, length us, event | category | flops | bytes accessed | tf_op | source)
XLA Modules:
  0.0 423.7 jit_solution(13524470347480903052)
XLA Ops:
  8.3 1.8 fusion.55
  10.2 2.1 fusion.54
  14.5 4.3 %select_select_fusion.2 = s32[256,1]{0,1:T(1,128)S(1)} fusion(s32[]{:T(128)} %bitcast.25, s32[]{:T(128)} %bitcast.26, s32[]{:T(128)} %bitcast.27, s32[]{:T(128)} %bitcast.28, s32[]{:T(128)} %bitcast.29, s32[]{:T(128)} %bitcast.31, s32[]{:T(128)} %bitcast.30), kind=kLoop, calls=%fused_computation.134 | loop fusion | flops 5888 | bytes 1052 | tf_op jit(solution)/shard_map/gather | solution.py:77
  18.8 15.7 %fusion.32 = (s32[256]{0:T(256)S(1)}, s32[256]{0:T(256)S(1)}) fusion(s32[256]{0:T(256)S(1)} %get-tuple-element.31, pred[256]{0:T(512)(128)(4,1)S(1)} %compare_reduce_fusion, pred[256]{0:T(512)(128)(4,1)S(1)} %compare_reduce_fusion.1, pred[256]{0:T(512)(128)(4,1)S(1)} %compare_reduce_fusion.2, pred[256]{0:T(512)(128)(4,1)S(1)} %compare_reduce_fusion.3, ...), kind=kLoop, calls=%fused_computation.129 | loop fusion | flops 9728 | bytes 10596 | tf_op jit(solution)/shard_map/add | solution.py:82
  34.8 1.4 scatter_custom_fusion.4
  39.2 1.5 scatter_custom_fusion.3
  41.3 4.4 %maximum_bitcast_fusion = bf16[4,1,147456]{2,0,1:T(4,128)(2,1)S(1)} fusion(bf16[4,16384]{1,0:T(4,128)(2,1)S(1)} %broadcast_select_fusion.1, bf16[4,131072]{1,0:T(4,128)(2,1)S(1)} %broadcast_select_fusion), kind=kLoop, calls=%fused_computation.33 | loop fusion | flops 2359296 | bytes 2359296 | tf_op jit(solution)/shard_map/all_to_all | solution.py:21
  46.3 2.1 reduce.50
  48.4 2.2 reshape.904
  50.7 5.0 %all-to-all-start = ((bf16[4,2,73728]{2,1,0:T(2,128)(2,1)}), bf16[4,2,73728]{2,1,0:T(2,128)(2,1)}, u32[]{:S(2)}, u32[]{:S(2)}) async-start(bf16[4,2,73728]{2,1,0:T(2,128)(2,1)} %reshape.904), calls=%async_computation | async-start | bytes 2359296 | tf_op jit(solution)/shard_map/all_to_all | solution.py:21
  55.7 1.6 scatter_custom_fusion.5
  57.4 12.5 %all-to-all-done = bf16[4,2,73728]{2,1,0:T(2,128)(2,1)} async-done(((bf16[4,2,73728]{2,1,0:T(2,128)(2,1)}), bf16[4,2,73728]{2,1,0:T(2,128)(2,1)}, u32[]{:S(2)}, u32[]{:S(2)}) %all-to-all-start) | async-done | bytes 1179680 | tf_op jit(solution)/shard_map/all_to_all | solution.py:21
  69.9 2.7 reshape.905
  72.6 2.5 copy.99
  82.9 4.3 %select_select_fusion.1 = s32[256,1]{0,1:T(1,128)S(1)} fusion(s32[]{:T(128)} %bitcast.61, s32[]{:T(128)} %bitcast.62, s32[]{:T(128)} %bitcast.63, s32[]{:T(128)} %bitcast.64, s32[]{:T(128)} %bitcast.65, s32[]{:T(128)} %bitcast.67, s32[]{:T(128)} %bitcast.66), kind=kLoop, calls=%fused_computation.133 | loop fusion | flops 5888 | bytes 1052 | tf_op jit(solution)/shard_map/gather | solution.py:103
  88.0 15.5 %select_select_fusion.3 = s32[256]{0:T(256)S(1)} fusion(pred[256]{0:T(512)(128)(4,1)S(1)} %compare_reduce_fusion, pred[256]{0:T(512)(128)(4,1)S(1)} %compare_reduce_fusion.1, pred[256]{0:T(512)(128)(4,1)S(1)} %compare_reduce_fusion.2, pred[256]{0:T(512)(128)(4,1)S(1)} %compare_reduce_fusion.3, pred[256]{0:T(512)(128)(4,1)S(1)} %compare_reduce_fusion.4, ...), kind=kLoop, calls=%fused_computation.135 | loop fusion | flops 6400 | bytes 8548 | tf_op jit(solution)/shard_map/gather | solution.py:103
  103.5 1.4 scatter_custom_fusion
  105.2 2.7 gather_fusion.3
  110.1 4.3 %select_select_fusion = s32[256,1]{0,1:T(1,128)S(1)} fusion(s32[]{:T(128)} %bitcast.96, s32[]{:T(128)} %bitcast.97, s32[]{:T(128)} %bitcast.98, s32[]{:T(128)} %bitcast.99, s32[]{:T(128)} %bitcast.100, s32[]{:T(128)} %bitcast.102, s32[]{:T(128)} %bitcast.101), kind=kLoop, calls=%fused_computation.132 | loop fusion | flops 5888 | bytes 1052 | tf_op jit(solution)/shard_map/gather | solution.py:86
  115.2 15.5 %fusion.37 = s32[256]{0:T(256)S(1)} fusion(pred[256]{0:T(512)(128)(4,1)S(1)} %compare_reduce_fusion, pred[256]{0:T(512)(128)(4,1)S(1)} %compare_reduce_fusion.1, pred[256]{0:T(512)(128)(4,1)S(1)} %compare_reduce_fusion.2, pred[256]{0:T(512)(128)(4,1)S(1)} %compare_reduce_fusion.3, pred[256]{0:T(512)(128)(4,1)S(1)} %compare_reduce_fusion.4, ...), kind=kLoop, calls=%fused_computation.139 | loop fusion | flops 8704 | bytes 8548 | tf_op jit(solution)/shard_map/jit(clip)/min | solution.py:86
  132.4 49.0 %all-gather.3.cloned.1.call-done = bf16[64,256,512]{2,1,0:T(8,128)(2,1)} async-done(((bf16[1,256,512]{2,1,0:T(8,128)(2,1)}), bf16[64,256,512]{2,1,0:T(8,128)(2,1)}) %all-gather.3.cloned.1.call-update) | async-done | bytes 16777232 | tf_op jit(solution)/shard_map/all_gather | solution.py:121
  181.4 11.6 %fusion.2 = f32[64,32,2,256]{3,1,2,0:T(8,128)} fusion(bf16[64,32,2,512]{3,1,2,0:T(8,128)(2,1)} %gather_fusion.3, bf16[64,256,512]{2,1,0:T(8,128)(2,1)} %all-gather.3.cloned.1.call-done), kind=kOutput, calls=%fused_computation.17 | convolution fusion | flops 1073741824 | bytes 25165824 | tf_op jit(solution)/shard_map/pqhc,pkc->pqhk/dot_general | solution.py:123
  193.0 65.4 %all-gather.5.cloned.1.call-done = bf16[64,64,256]{2,1,0:T(8,128)(2,1)} async-done(((bf16[1,64,256]{2,1,0:T(8,128)(2,1)}), bf16[64,64,256]{2,1,0:T(8,128)(2,1)}) %all-gather.5.cloned.1.call-update) | async-done | bytes 2097168 | tf_op jit(solution)/shard_map/all_gather | solution.py:122
  258.4 5.7 %fusion.56 = (f32[64,32,2]{1,2,0:T(2,128)S(1)}, f32[64,32,2,256]{3,1,2,0:T(8,128)}) fusion(f32[64,32,2,256]{3,1,2,0:T(8,128)} %fusion.2, bf16[64,32,2,64]{3,1,2,0:T(8,128)(2,1)S(1)} %gather_fusion.7, bf16[64,64,256]{2,1,0:T(8,128)(2,1)} %all-gather.5.cloned.1.call-done, pred[64,256]{1,0:T(8,128)(4,1)S(1)} %iota_compare_fusion.1), kind=kOutput, calls=%fused_computation.171 | convolution fusion | flops 138407936 | bytes 11042816 | tf_op jit(solution)/shard_map/pqhr,prk->pqhk/dot_general | solution.py:126
  265.1 3.2 fusion.6
  268.5 9.6 %fusion = f32[64,32,2,512]{3,1,2,0:T(8,128)S(1)} fusion(bf16[64,256,512]{2,1,0:T(8,128)(2,1)} %all-gather.3.cloned.1.call-done, f32[64,32,2,256]{3,1,2,0:T(8,128)} %get-tuple-element.136, f32[64,32,2]{1,2,0:T(2,128)S(1)} %gather_fusion.8, pred[64,256]{1,0:T(8,128)(4,1)S(1)} %iota_compare_fusion.1), kind=kOutput, calls=%fused_computation.15 | convolution fusion | flops 1076887552 | bytes 29392896 | tf_op jit(solution)/shard_map/pqhk,pkc->pqhc/dot_general | solution.py:141
  278.1 7.5 %fusion.16 = bf16[8,32,2,512]{3,0,2,1:T(8,128)(2,1)S(1)} fusion(f32[64,32,2,512]{3,1,2,0:T(8,128)S(1)} %fusion, f32[8,32,2]{0,2,1:T(2,128)S(1)} %copy.61, s32[64]{0:T(128)S(1)} %get-tuple-element.37), kind=kOutput, calls=%fused_computation.31 | convolution fusion | flops 201851392 | bytes 8915200 | tf_op jit(solution)/shard_map/pr,pqhc->rqhc/dot_general | solution.py:147
  286.3 4.1 convolution_bitcast_fusion
  290.5 82.5 %reduce-scatter.8.cloned.1.call-done = f32[896,256]{0,1:T(8,128)} async-done(((f32[7168,256]{0,1:T(8,128)}), f32[896,256]{0,1:T(8,128)}) %reduce-scatter.8.cloned.1.call-update) | async-done | bytes 917520 | tf_op jit(solution)/shard_map/reduce_scatter | solution.py:30
  372.9 2.4 copy.69
  375.4 22.8 %reduce-scatter.10.cloned.1.call-done = f32[224,256]{1,0:T(8,128)} async-done(((f32[896,256]{1,0:T(8,128)}), f32[224,256]{1,0:T(8,128)}) %reduce-scatter.10.cloned.1.call-update) | async-done | bytes 229392
  398.2 17.2 %reduce-scatter.12.cloned.1.call-done = f32[112,256]{1,0:T(8,128)} async-done(((f32[224,256]{1,0:T(8,128)}), f32[112,256]{1,0:T(8,128)}) %reduce-scatter.12.cloned.1.call-update) | async-done | bytes 114704
  (114 shorter events, 25.1 us)
Async XLA Ops:
  6.5 31.2 %copy-start = (bf16[2,256,512]{2,1,0:T(8,128)(2,1)S(1)}, bf16[2,256,512]{2,1,0:T(8,128)(2,1)}, u32[]{:S(2)}) copy-start(bf16[2,256,512]{2,1,0:T(8,128)(2,1)} %param.11) | copy-start | bytes 1572868
  50.7 19.2 %all-to-all-start = ((bf16[4,2,73728]{2,1,0:T(2,128)(2,1)}), bf16[4,2,73728]{2,1,0:T(2,128)(2,1)}, u32[]{:S(2)}, u32[]{:S(2)}) async-start(bf16[4,2,73728]{2,1,0:T(2,128)(2,1)} %reshape.904), calls=%async_computation | async-start | bytes 2359296 | tf_op jit(solution)/shard_map/all_to_all | solution.py:21
  55.7 125.7 %all-gather.3.cloned.1.call-start = ((), (), s32[]{:S(2)}) async-start(), calls=%async_computation.4 | async-start | bytes 17039360 | tf_op jit(solution)/shard_map/all_gather | solution.py:121
  72.6 7.4 %copy-start.5 = (bf16[1024,256]{1,0:T(8,128)(2,1)S(1)}, bf16[1024,256]{1,0:T(8,128)(2,1)}, u32[]{:S(2)}) copy-start(bf16[1024,256]{1,0:T(8,128)(2,1)} %param.13) | copy-start | bytes 1572868
  75.1 1.0 copy-start.3
  75.1 6.1 %copy-start.6 = (bf16[1024,128]{1,0:T(8,128)(2,1)S(1)}, bf16[1024,128]{1,0:T(8,128)(2,1)}, u32[]{:S(2)}) copy-start(bf16[1024,128]{1,0:T(8,128)(2,1)} %param.14) | copy-start | bytes 786436
  75.2 29.7 %copy-start.7 = (bf16[512,256]{1,0:T(8,128)(2,1)S(1)}, bf16[512,256]{1,0:T(8,128)(2,1)}, u32[]{:S(2)}) copy-start(bf16[512,256]{1,0:T(8,128)(2,1)} %param.15) | copy-start | bytes 786436
  77.5 180.9 %all-gather.5.cloned.1.call-start = ((), (), s32[]{:S(2)}) async-start(), calls=%async_computation.5 | async-start | bytes 2129920 | tf_op jit(solution)/shard_map/all_gather | solution.py:122
  79.1 293.8 %reduce-scatter.8.cloned.1.call-start = ((), (), s32[]{:S(2)}) async-start(), calls=%async_computation.6 | async-start | bytes 8257536 | tf_op jit(solution)/shard_map/reduce_scatter | solution.py:30
  105.2 3.5 copy-start.2
  105.2 26.9 %copy-start.8 = (bf16[512,256]{1,0:T(8,128)(2,1)S(1)}, bf16[512,256]{1,0:T(8,128)(2,1)}, u32[]{:S(2)}) copy-start(bf16[512,256]{1,0:T(8,128)(2,1)} %param.16) | copy-start | bytes 786436
  278.1 8.1 %copy-start.4 = (bf16[256,7168]{1,0:T(8,128)(2,1)S(1)}, bf16[256,7168]{1,0:T(8,128)(2,1)}, u32[]{:S(2)}) copy-start(bf16[256,7168]{1,0:T(8,128)(2,1)} %param.17) | copy-start | bytes 11010052
  290.4 126.8 %copy-start.1 = (bf16[2,256,512]{2,1,0:T(8,128)(2,1)S(1)}, bf16[2,256,512]{2,1,0:T(8,128)(2,1)}, u32[]{:S(2)}) copy-start(bf16[2,256,512]{2,1,0:T(8,128)(2,1)} %param.11) | copy-start | bytes 1572868
  290.4 107.8 %reduce-scatter.10.cloned.1.call-start = ((), (), s32[]{:S(2)}) async-start(), calls=%async_computation.7 | async-start | bytes 1146880
  375.4 40.1 %reduce-scatter.12.cloned.1.call-start = ((), (), s32[]{:S(2)}) async-start(), calls=%async_computation.8 | async-start | bytes 344064
Sparse Core Ops, SparseCore 0:
  77.6 103.7 all-gather.2
  184.1 74.2 all-gather.4
  290.5 82.3 reduce-scatter.7
  375.5 22.6 reduce-scatter.9
  400.6 14.8 reduce-scatter.11
where the time goes:
time: 425 us; the launch traced here: 424 us
  waiting for transfers between devices  249 us (59%)
  other arithmetic  73.1 us (17%)
  local copies, waits for them, and re-layouts  42.8 us (10%)
  matrix products  39.3 us (9%)
  between operations  13.8 us (3%)
  starting transfers between devices  5.18 us (1%)
    reduce_scatter x1, waiting for transfers between devices, summed_rows(): so_far = lax.psum_scatter(so_far, axis, scatter_dimension=0, tiled=True)  82.5 us
    all_gather x1, waiting for transfers between devices, local(): rope_piece = lax.all_gather(own_rope, DEV, axis=0, tiled=True)  65.4 us
    all_gather x1, waiting for transfers between devices, local(): latent_piece = lax.all_gather(own_latent, DEV, axis=0, tiled=True)  49 us
    unnamed x7, waiting for transfers between devices  40.1 us
    gather x2, other arithmetic, local(): page_req = place_values(pos_target, rank[entry_req], group_pages, jnp.int32)  19.8 us
    add x1, other arithmetic, local(): entry_key = entry_col * groups + entry_group  15.7 us
    min x1, other arithmetic, local(): entry_valid = jnp.clip(slot_len[entry_req] - entry_block * block, 0, block)  15.5 us
    unnamed x28, local copies, waits for them, and re-layouts  13.8 us
  transfers between devices with their start and end apart: 6, of which 6 were waited for; matrix products, arithmetic and copies ran while one was open for 16% of the time, Pallas kernels for 0%

commit v1 on v0

--- a/solution.py
+++ b/solution.py
@@ -118,7 +118,9 @@
     request_ids = jnp.arange(per_group, dtype=jnp.int32)
     token_ids = jnp.arange(block, dtype=jnp.int32)
     start_top = jnp.full((per_group, query_rows, heads_dev), NEG, jnp.float32)
-    latent_piece = lax.all_gather(own_latent, DEV, axis=0, tiled=True)
+    latent_piece = jnp.concatenate(
+        lax.all_to_all(jnp.stack([own_latent] * lax.axis_size(DEV)), DEV, 0, 0), axis=0
+    )
     rope_piece = lax.all_gather(own_rope, DEV, axis=0, tiled=True)
     score = jnp.einsum(
         "pqhc,pkc->pqhk", q_lat[page_req], latent_piece, preferred_element_type=jnp.float32

time: 425 us -> 652 us (1.53)
  waiting for transfers between devices: 249 us -> 457 us
  starting transfers between devices: 5.18 us -> 20.4 us
    all_to_all x0 -> x1, waiting for transfers between devices: none -> 314 us  [local(): lax.all_to_all(jnp.stack([own_latent] * lax.axis_size(DEV)), DEV, 0, 0)]
    all_gather x1, waiting for transfers between devices: 65.4 us -> 0.01 us  [local(): rope_piece = lax.all_gather(own_rope, DEV, axis=0, tiled=True)]
    all_gather x1 -> x0, waiting for transfers between devices: 49 us -> none  [local(): latent_piece = lax.all_gather(own_latent, DEV, axis=0, tiled=True)]
    all_to_all x0 -> x1, starting transfers between devices: none -> 15.2 us  [local(): lax.all_to_all(jnp.stack([own_latent] * lax.axis_size(DEV)), DEV, 0, 0)]
    reduce_scatter x1, waiting for transfers between devices: 82.5 us -> 90.9 us  [summed_rows(): so_far = lax.psum_scatter(so_far, axis, scatter_dimension=0, tiled=True)]
    unnamed x28 -> x30, local copies, waits for them, and re-layouts: 13.8 us -> 13.8 us
    unnamed x7 -> x6, waiting for transfers between devices: 40.1 us -> 40.1 us
  transfers between devices with their start and end apart: 6 -> 6, of which waited for: 6 -> 5; matrix products, arithmetic and copies ran while one was open for 16% -> 10% of each run, Pallas kernels for 0% -> 0%
where the time goes in v1:
time: 652 us; the launch traced here: 650 us
  waiting for transfers between devices  457 us (70%)
  other arithmetic  72.2 us (11%)
  local copies, waits for them, and re-layouts  47.4 us (7%)
  matrix products  39.2 us (6%)
  starting transfers between devices  20.4 us (3%)
  between operations  13.8 us (2%)
    all_to_all x1, waiting for transfers between devices, local(): lax.all_to_all(jnp.stack([own_latent] * lax.axis_size(DEV)), DEV, 0, 0)  314 us
    reduce_scatter x1, waiting for transfers between devices, summed_rows(): so_far = lax.psum_scatter(so_far, axis, scatter_dimension=0, tiled=True)  90.9 us
    unnamed x6, waiting for transfers between devices  40.1 us
    gather x2, other arithmetic, local(): page_req = place_values(pos_target, rank[entry_req], group_pages, jnp.int32)  19.3 us
    add x1, other arithmetic, local(): entry_key = entry_col * groups + entry_group  15.7 us
    all_to_all x1, starting transfers between devices, local(): lax.all_to_all(jnp.stack([own_latent] * lax.axis_size(DEV)), DEV, 0, 0)  15.2 us
    min x1, other arithmetic, local(): entry_valid = jnp.clip(slot_len[entry_req] - entry_block * block, 0, block)  15.1 us
    unnamed x30, local copies, waits for them, and re-layouts  13.8 us
  transfers between devices with their start and end apart: 6, of which 5 were waited for; matrix products, arithmetic and copies ran while one was open for 10% of the time, Pallas kernels for 0%

profile of v1, /device:TPU:1, one launch (start us, length us, event | category | flops | bytes accessed | tf_op | source)
XLA Modules:
  0.0 650.4 jit_solution(13827955965876753969)
XLA Ops:
  6.5 1.8 fusion.55
  8.4 2.1 fusion.54
  14.5 4.3 select_select_fusion.2
  18.8 15.7 %fusion.32 = (s32[256]{0:T(256)S(1)}, s32[256]{0:T(256)S(1)}) fusion(s32[256]{0:T(256)S(1)} %get-tuple-element.31, pred[256]{0:T(512)(128)(4,1)S(1)} %compare_reduce_fusion, pred[256]{0:T(512)(128)(4,1)S(1)} %compare_reduce_fusion.1, pred[256]{0:T(512)(128)(4,1)S(1)} %compare_reduce_fusion.2, pred[256]{0:T(512)(128)(4,1)S(1)} %compare_reduce_fusion.3, ...), kind=kLoop, calls=%fused_computation.130 | loop fusion | flops 9728 | bytes 10596 | tf_op jit(solution)/shard_map/add | solution.py:82
  34.8 1.4 scatter_custom_fusion.4
  38.4 1.5 scatter_custom_fusion.3
  40.5 4.4 maximum_bitcast_fusion
  45.5 2.1 reduce.50
  47.6 2.2 reshape.911
  49.9 5.0 all-to-all-start
  54.9 1.6 scatter_custom_fusion.5
  56.6 12.5 %all-to-all-done = bf16[4,2,73728]{2,1,0:T(2,128)(2,1)} async-done(((bf16[4,2,73728]{2,1,0:T(2,128)(2,1)}), bf16[4,2,73728]{2,1,0:T(2,128)(2,1)}, u32[]{:S(2)}, u32[]{:S(2)}) %all-to-all-start) | async-done | bytes 1179680 | tf_op jit(solution)/shard_map/all_to_all | solution.py:21
  69.1 2.7 reshape.912
  71.8 2.5 copy.99
  75.9 6.0 stack.2
  81.9 15.2 %all-to-all-start.1 = ((bf16[64,1,256,512]{3,2,1,0:T(8,128)(2,1)}), bf16[64,1,256,512]{3,2,1,0:T(8,128)(2,1)}, u32[]{:S(2)}, u32[]{:S(2)}) async-start(bf16[64,1,256,512]{3,2,1,0:T(8,128)(2,1)} %stack.2), calls=%async_computation.1 | async-start | bytes 33554432 | tf_op jit(solution)/shard_map/all_to_all | solution.py:122
  102.6 4.1 select_select_fusion.1
  107.4 15.2 %select_select_fusion.3 = s32[256]{0:T(256)S(1)} fusion(pred[256]{0:T(512)(128)(4,1)S(1)} %compare_reduce_fusion, pred[256]{0:T(512)(128)(4,1)S(1)} %compare_reduce_fusion.1, pred[256]{0:T(512)(128)(4,1)S(1)} %compare_reduce_fusion.2, pred[256]{0:T(512)(128)(4,1)S(1)} %compare_reduce_fusion.3, pred[256]{0:T(512)(128)(4,1)S(1)} %compare_reduce_fusion.4, ...), kind=kLoop, calls=%fused_computation.136 | loop fusion | flops 6400 | bytes 8548 | tf_op jit(solution)/shard_map/gather | solution.py:103
  124.4 2.9 gather_fusion.3
  129.4 4.3 select_select_fusion
  134.4 15.1 %fusion.37 = s32[256]{0:T(256)S(1)} fusion(pred[256]{0:T(512)(128)(4,1)S(1)} %compare_reduce_fusion, pred[256]{0:T(512)(128)(4,1)S(1)} %compare_reduce_fusion.1, pred[256]{0:T(512)(128)(4,1)S(1)} %compare_reduce_fusion.2, pred[256]{0:T(512)(128)(4,1)S(1)} %compare_reduce_fusion.3, pred[256]{0:T(512)(128)(4,1)S(1)} %compare_reduce_fusion.4, ...), kind=kLoop, calls=%fused_computation.140 | loop fusion | flops 8704 | bytes 8548 | tf_op jit(solution)/shard_map/jit(clip)/min | solution.py:86
  151.2 313.9 %all-to-all-done.1 = bf16[64,1,256,512]{3,2,1,0:T(8,128)(2,1)} async-done(((bf16[64,1,256,512]{3,2,1,0:T(8,128)(2,1)}), bf16[64,1,256,512]{3,2,1,0:T(8,128)(2,1)}, u32[]{:S(2)}, u32[]{:S(2)}) %all-to-all-start.1) | async-done | bytes 16777248 | tf_op jit(solution)/shard_map/all_to_all | solution.py:122
  465.1 11.6 %fusion.2 = f32[64,32,2,256]{3,1,2,0:T(8,128)} fusion(bf16[64,32,2,512]{3,1,2,0:T(8,128)(2,1)} %gather_fusion.3, bf16[64,1,256,512]{3,2,1,0:T(8,128)(2,1)} %all-to-all-done.1), kind=kOutput, calls=%fused_computation.17 | convolution fusion | flops 1073741824 | bytes 25165824 | tf_op jit(solution)/shard_map/pqhc,pkc->pqhk/dot_general | solution.py:125
  476.7 5.7 fusion.56
  483.3 3.2 fusion.6
  486.7 9.6 %fusion = f32[64,32,2,512]{3,1,2,0:T(8,128)S(1)} fusion(bf16[64,1,256,512]{3,2,1,0:T(8,128)(2,1)} %all-to-all-done.1, f32[64,32,2,256]{3,1,2,0:T(8,128)} %get-tuple-element.136, f32[64,32,2]{1,2,0:T(2,128)S(1)} %gather_fusion.8, pred[64,256]{1,0:T(8,128)(4,1)S(1)} %iota_compare_fusion.1), kind=kOutput, calls=%fused_computation.15 | convolution fusion | flops 1076887552 | bytes 29392896 | tf_op jit(solution)/shard_map/pqhk,pkc->pqhc/dot_general | solution.py:143
  496.4 7.5 %fusion.16 = bf16[8,32,2,512]{3,0,2,1:T(8,128)(2,1)S(1)} fusion(f32[64,32,2,512]{3,1,2,0:T(8,128)S(1)} %fusion, f32[8,32,2]{0,2,1:T(2,128)S(1)} %copy.61, s32[64]{0:T(128)S(1)} %get-tuple-element.37), kind=kOutput, calls=%fused_computation.31 | convolution fusion | flops 201851392 | bytes 8915200 | tf_op jit(solution)/shard_map/pr,pqhc->rqhc/dot_general | solution.py:149
  504.5 4.1 convolution_bitcast_fusion
  508.7 90.9 %reduce-scatter.8.cloned.1.call-done = f32[896,256]{0,1:T(8,128)} async-done(((f32[7168,256]{0,1:T(8,128)}), f32[896,256]{0,1:T(8,128)}) %reduce-scatter.8.cloned.1.call-update) | async-done | bytes 917520 | tf_op jit(solution)/shard_map/reduce_scatter | solution.py:30
  599.6 2.4 copy.69
  602.1 22.7 %reduce-scatter.10.cloned.1.call-done = f32[224,256]{1,0:T(8,128)} async-done(((f32[896,256]{1,0:T(8,128)}), f32[224,256]{1,0:T(8,128)}) %reduce-scatter.10.cloned.1.call-update) | async-done | bytes 229392
  624.7 17.4 %reduce-scatter.12.cloned.1.call-done = f32[112,256]{1,0:T(8,128)} async-done(((f32[224,256]{1,0:T(8,128)}), f32[112,256]{1,0:T(8,128)}) %reduce-scatter.12.cloned.1.call-update) | async-done | bytes 114704
  (116 shorter events, 25.0 us)
Async XLA Ops:
  6.5 29.7 %copy-start = (bf16[2,256,512]{2,1,0:T(8,128)(2,1)S(1)}, bf16[2,256,512]{2,1,0:T(8,128)(2,1)}, u32[]{:S(2)}) copy-start(bf16[2,256,512]{2,1,0:T(8,128)(2,1)} %param.11) | copy-start | bytes 1572868
  6.5 31.2 %copy-start.9 = (bf16[2,64,256]{2,1,0:T(8,128)(2,1)S(1)}, bf16[2,64,256]{2,1,0:T(8,128)(2,1)}, u32[]{:S(2)}) copy-start(bf16[2,64,256]{2,1,0:T(8,128)(2,1)} %param.12) | copy-start | bytes 196612
  49.9 19.2 %all-to-all-start = ((bf16[4,2,73728]{2,1,0:T(2,128)(2,1)}), bf16[4,2,73728]{2,1,0:T(2,128)(2,1)}, u32[]{:S(2)}, u32[]{:S(2)}) async-start(bf16[4,2,73728]{2,1,0:T(2,128)(2,1)} %reshape.911), calls=%async_computation | async-start | bytes 2359296 | tf_op jit(solution)/shard_map/all_to_all | solution.py:21
  74.3 1.0 copy-start.3
  81.9 17.8 %copy-start.5 = (bf16[1024,256]{1,0:T(8,128)(2,1)S(1)}, bf16[1024,256]{1,0:T(8,128)(2,1)}, u32[]{:S(2)}) copy-start(bf16[1024,256]{1,0:T(8,128)(2,1)} %param.13) | copy-start | bytes 1572868
  81.9 19.0 %copy-start.6 = (bf16[1024,128]{1,0:T(8,128)(2,1)S(1)}, bf16[1024,128]{1,0:T(8,128)(2,1)}, u32[]{:S(2)}) copy-start(bf16[1024,128]{1,0:T(8,128)(2,1)} %param.14) | copy-start | bytes 786436
  81.9 42.2 %copy-start.7 = (bf16[512,256]{1,0:T(8,128)(2,1)S(1)}, bf16[512,256]{1,0:T(8,128)(2,1)}, u32[]{:S(2)}) copy-start(bf16[512,256]{1,0:T(8,128)(2,1)} %param.15) | copy-start | bytes 786436
  81.9 383.2 %all-to-all-start.1 = ((bf16[64,1,256,512]{3,2,1,0:T(8,128)(2,1)}), bf16[64,1,256,512]{3,2,1,0:T(8,128)(2,1)}, u32[]{:S(2)}, u32[]{:S(2)}) async-start(bf16[64,1,256,512]{3,2,1,0:T(8,128)(2,1)} %stack.2), calls=%async_computation.1 | async-start | bytes 33554432 | tf_op jit(solution)/shard_map/all_to_all | solution.py:122
  97.1 379.6 %all-gather.2.cloned.1.call-start = ((), (), s32[]{:S(2)}) async-start(), calls=%async_computation.5 | async-start | bytes 2129920 | tf_op jit(solution)/shard_map/all_gather | solution.py:124
  98.8 500.8 %reduce-scatter.8.cloned.1.call-start = ((), (), s32[]{:S(2)}) async-start(), calls=%async_computation.6 | async-start | bytes 8257536 | tf_op jit(solution)/shard_map/reduce_scatter | solution.py:30
  124.4 3.6 copy-start.2
  124.4 26.6 %copy-start.8 = (bf16[512,256]{1,0:T(8,128)(2,1)S(1)}, bf16[512,256]{1,0:T(8,128)(2,1)}, u32[]{:S(2)}) copy-start(bf16[512,256]{1,0:T(8,128)(2,1)} %param.16) | copy-start | bytes 786436
  496.3 8.1 %copy-start.4 = (bf16[256,7168]{1,0:T(8,128)(2,1)S(1)}, bf16[256,7168]{1,0:T(8,128)(2,1)}, u32[]{:S(2)}) copy-start(bf16[256,7168]{1,0:T(8,128)(2,1)} %param.17) | copy-start | bytes 11010052
  508.6 135.3 %copy-start.1 = (bf16[2,256,512]{2,1,0:T(8,128)(2,1)S(1)}, bf16[2,256,512]{2,1,0:T(8,128)(2,1)}, u32[]{:S(2)}) copy-start(bf16[2,256,512]{2,1,0:T(8,128)(2,1)} %param.11) | copy-start | bytes 1572868
  508.6 116.1 %reduce-scatter.10.cloned.1.call-start = ((), (), s32[]{:S(2)}) async-start(), calls=%async_computation.7 | async-start | bytes 1146880
  602.0 40.1 %reduce-scatter.12.cloned.1.call-start = ((), (), s32[]{:S(2)}) async-start(), calls=%async_computation.8 | async-start | bytes 344064
Sparse Core Ops, SparseCore 0:
  100.7 136.1 all-gather.1
  508.7 90.7 reduce-scatter.7
  602.1 22.5 reduce-scatter.9
  627.1 15.0 reduce-scatter.11
